TPU v7x, 32 devices: a whole 2x2x4 slice. The times are simulated.
32 devices in a mesh: row: 4 (over z), col: 8 (over y, x, core).
Axes of the slice: x: 2, y: 2, z: 4, core: 2. Of those that a mesh axis runs over, the one named last changes fastest.
Arguments:
- pencil_a: float32 [4, 3072, 8, 1536], P('row', None, 'col'), may hold values from -6 to 6, as said below
- pencil_b: float32 [4, 3072, 8, 1536], P('row', None, 'col'), may hold values from -6 to 6
Outputs:
- new_a: float32 [4, 3072, 8, 1536], P('row', None, 'col')
- new_b: float32 [4, 3072, 8, 1536], P('row', None, 'col')
Inputs may be any that keep to these rules, and one draw needn't show every extreme that they name: `pencil_a`: the first 256 columns of Amat are zero in the last 256 rows of Amat.
All inputs are finite; a program needn't handle non-finite values.
Results may differ from a plain program's by a relative error of at most 0.000056.
Values sent between devices are 32-bit elements; how exact they have to be, the bound alone decides.
A program may use at most 192 MiB of HBM per device.

v0:
```python
import jax
import jax.numpy as jnp
from jax import lax
from jax.sharding import PartitionSpec as P

NB = 256


def broadcast(array, axis, root):
    mine = lax.axis_index(axis) == root
    return lax.psum(jnp.where(mine, array, jnp.zeros_like(array)), axis)


def matmul(left, right):
    return jnp.dot(left, right, precision=lax.Precision.HIGHEST, preferred_element_type=jnp.float32)


def inverse_factor(gram):
    lower = jnp.linalg.cholesky(gram)
    ident = jnp.eye(gram.shape[0], dtype=jnp.float32)
    return jax.scipy.linalg.solve_triangular(lower, ident, lower=True).T


def general_inverse(square):
    lower = jnp.linalg.cholesky(matmul(square, square.T))
    ident = jnp.eye(square.shape[0], dtype=jnp.float32)
    linv = jax.scipy.linalg.solve_triangular(lower, ident, lower=True)
    return matmul(square.T, matmul(linv.T, linv))


def fast_matmul(left, right):
    return jnp.dot(left, right, precision=lax.Precision.HIGH, preferred_element_type=jnp.float32)


def on_device(pencil_a, pencil_b):
    rows_loc = pencil_a.shape[1]
    cols_loc = pencil_a.shape[3]
    amat = pencil_a.reshape(rows_loc, cols_loc)
    bmat = pencil_b.reshape(rows_loc, cols_loc)
    width = NB
    ident = jnp.eye(width, dtype=jnp.float32)
    row = lax.axis_index("row")
    col = lax.axis_index("col")
    last_row = lax.axis_size("row") - 1
    last_col = lax.axis_size("col") - 1
    top_mask = (row == 0).astype(jnp.float32)
    end_mask = (col == last_col).astype(jnp.float32)
    own_panel = amat[:, :width]
    own_strip = bmat[rows_loc - width :]
    zero = jnp.zeros((width, width), jnp.float32)
    small = jnp.stack(
        [
            jnp.where(col == 0, matmul(own_panel.T, own_panel), zero),
            jnp.where((col == 0) & (row == 0), own_panel[:width], zero),
            jnp.where(row == last_row, matmul(own_strip, own_strip.T), zero),
            jnp.where((col == last_col) & (row == last_row), own_strip[:, cols_loc - width :], zero),
        ]
    )
    small = lax.psum(small, ("row", "col"))
    own_panel, own_strip, small = lax.optimization_barrier((own_panel, own_strip, small))
    panel = broadcast(own_panel, "col", 0)
    strip = broadcast(own_strip, "row", last_row)
    left_inv = inverse_factor(small[0])
    right_inv = inverse_factor(small[2])
    vectors = matmul(panel, left_inv) + top_mask * jnp.pad(ident, ((0, rows_loc - width), (0, 0)))
    vectors_t = matmul(right_inv.T, strip) + end_mask * jnp.pad(
        ident, ((0, 0), (cols_loc - width, 0))
    )
    vectors, strip = lax.optimization_barrier((vectors, strip))
    products_a, products_b = lax.psum(
        (fast_matmul(vectors.T, amat), fast_matmul(vectors.T, bmat)), "row"
    )
    share = lax.psum_scatter(
        jnp.concatenate([fast_matmul(amat, vectors_t.T), fast_matmul(bmat, vectors_t.T)], axis=1),
        "col",
        scatter_dimension=0,
        tiled=True,
    )
    kinv_right = general_inverse(ident + matmul(right_inv.T, small[3]).T)
    kinv_left = general_inverse(ident + matmul(small[1], left_inv))
    scaled = jnp.concatenate(
        [matmul(share[:, :width], kinv_right.T), matmul(share[:, width:], kinv_right.T)], axis=1
    )
    gathered = lax.all_gather(scaled, "col", axis=0, tiled=True)
    cross = lax.psum(
        jnp.concatenate([matmul(products_a, vectors_t.T), matmul(products_b, vectors_t.T)], axis=0),
        "col",
    )

    def update(matrix, products, mixed, crossed):
        inner = products - matmul(matmul(crossed, kinv_right.T), vectors_t)
        low = jnp.concatenate([matmul(kinv_left, inner), vectors_t], axis=0)
        return matrix - fast_matmul(jnp.concatenate([vectors, mixed], axis=1), low)

    amat = update(amat, products_a, gathered[:, :width], cross[:width])
    bmat = update(bmat, products_b, gathered[:, width:], cross[width:])
    return (amat.reshape(1, rows_loc, 1, cols_loc), bmat.reshape(1, rows_loc, 1, cols_loc))


def solution(mesh):
    placed = (P("row", None, "col", None), P("row", None, "col", None))
    return jax.shard_map(
        on_device,
        mesh=mesh,
        in_specs=placed,
        out_specs=(P("row", None, "col", None), P("row", None, "col", None)),
        check_vma=False,
    )
```

profile of v0, /device:TPU:0, one launch (start us, length us, event | category | flops | bytes accessed | tf_op | source)
XLA Modules:
  0.0 798.0 jit_solution(4191456055535194326)
XLA Ops:
  7.2 1.3 slice-done
  8.6 1.4 copy.23
  10.0 2.6 fusion.14
  12.6 39.6 %copy.4 = f32[1,3072,1,1536]{1,3,2,0:T(8,128)} copy(f32[1,3072,1,1536]{3,2,1,0:T(1,128)} %param.5) | data formatting | bytes 37748736 | tf_op args[0]
  52.3 5.5 fusion.15
  60.0 3.9 slice.111
  63.9 129.5 %all-reduce.10.cloned.1.call-done = f32[4,256,256]{1,2,0:T(8,128)} async-done(((f32[4,256,256]{1,2,0:T(8,128)}), f32[4,256,256]{1,2,0:T(8,128)}) %all-reduce.10.cloned.1.call-update) | async-done | bytes 1048592 | tf_op jit(solution)/shard_map/psum | solution.py:59
  193.4 3.9 broadcast_select_fusion
  201.9 11.7 %cholesky.248 = f32[128,128]{1,0:T(8,128)S(1)} custom-call(f32[128,128]{1,0:T(8,128)S(1)} %cholesky.349), custom_call_target="Cholesky" | custom-call | tf_op jit(solution)/shard_map/jit(cholesky)/cholesky | solution.py:19
  214.5 11.7 %cholesky.214 = f32[128,128]{1,0:T(8,128)S(1)} custom-call(f32[128,128]{1,0:T(8,128)S(1)} %cholesky.346), custom_call_target="Cholesky" | custom-call | tf_op jit(solution)/shard_map/jit(cholesky)/cholesky | solution.py:19
  226.9 9.8 %custom-call.17 = f32[1,128,128]{1,2,0:T(8,128)S(1)} custom-call(f32[1,128,128]{2,1,0:T(8,128)S(1)} %get-tuple-element.107), custom_call_target="InvertDiagBlocksLowerTriangular" | custom-call | tf_op jit(solution)/shard_map/jit(cholesky)/cholesky | solution.py:19
  237.4 10.0 %custom-call.19 = f32[1,128,128]{1,2,0:T(8,128)S(1)} custom-call(f32[1,128,128]{2,1,0:T(8,128)S(1)} %get-tuple-element.103), custom_call_target="InvertDiagBlocksLowerTriangular" | custom-call | tf_op jit(solution)/shard_map/jit(cholesky)/cholesky | solution.py:19
  249.6 11.7 %cholesky.265 = f32[128,128]{1,0:T(8,128)S(1)} custom-call(f32[128,128]{1,0:T(8,128)S(1)} %convolution_subtract_fusion.8), custom_call_target="Cholesky" | custom-call | tf_op jit(solution)/shard_map/jit(cholesky)/cholesky | solution.py:19
  264.2 11.7 %cholesky.231 = f32[128,128]{1,0:T(8,128)S(1)} custom-call(f32[128,128]{1,0:T(8,128)S(1)} %convolution_subtract_fusion.9), custom_call_target="Cholesky" | custom-call | tf_op jit(solution)/shard_map/jit(cholesky)/cholesky | solution.py:19
  280.5 4.0 while.9
  281.1 1.3 bitcast_dynamic-update-slice_fusion.9
  283.1 1.3 bitcast_dynamic-update-slice_fusion.9
  284.9 3.9 while.8
  287.5 1.3 bitcast_dynamic-update-slice_fusion.8
  288.8 19.7 %custom-call.20 = f32[2,128,128]{1,2,0:T(8,128)S(1)} custom-call(f32[2,128,128]{2,1,0:T(8,128)S(1)} %get-tuple-element.39), custom_call_target="InvertDiagBlocksLowerTriangular" | custom-call | tf_op jit(solution)/shard_map/jit(_solve_triangular)/triangular_solve | solution.py:21
  308.5 19.7 %custom-call.18 = f32[2,128,128]{1,2,0:T(8,128)S(1)} custom-call(f32[2,128,128]{2,1,0:T(8,128)S(1)} %get-tuple-element.38), custom_call_target="InvertDiagBlocksLowerTriangular" | custom-call | tf_op jit(solution)/shard_map/jit(_solve_triangular)/triangular_solve | solution.py:21
  330.7 7.0 convolution_add_fusion
  337.7 14.5 %all-reduce.14.cloned.1.call-done = f32[256,1536]{0,1:T(8,128)} async-done(((f32[256,1536]{0,1:T(8,128)}), f32[256,1536]{0,1:T(8,128)}) %all-reduce.14.cloned.1.call-update) | async-done | bytes 1572880 | tf_op jit(solution)/shard_map/psum | solution.py:11
  352.2 17.5 %fusion = f32[256,1536]{1,0:T(8,128)} fusion(f32[3072,256]{1,0:T(8,128)S(1)} %convolution_add_fusion, f32[1,3072,1,1536]{3,2,1,0:T(1,128)} %param.6), kind=kOutput, calls=%fused_computation.9 | convolution fusion | flops 7247757312 | bytes 23592960 | tf_op jit(solution)/shard_map/dot_general | solution.py:32
  369.6 19.3 %fusion.80 = f32[256,1536]{1,0:T(8,128)} fusion(f32[3072,256]{1,0:T(8,128)S(1)} %convolution_add_fusion, f32[1,3072,1,1536]{1,3,2,0:T(8,128)} %copy.4), kind=kOutput, calls=%fused_computation.170 | convolution fusion | flops 7247757312 | bytes 23592960 | tf_op jit(solution)/shard_map/dot_general | solution.py:32
  391.2 2.9 convolution_add_fusion.1
  394.2 15.4 %fusion.9 = f32[3072,256]{0,1:T(8,128)S(1)} fusion(f32[256,1536]{1,0:T(8,128)S(1)} %convolution_add_fusion.1, f32[1,3072,1,1536]{3,2,1,0:T(1,128)} %param.6), kind=kOutput, calls=%fused_computation.22 | convolution fusion | flops 7247757312 | bytes 23592960 | tf_op jit(solution)/shard_map/dot_general | solution.py:32
  409.6 11.9 %convolution_bitcast_fusion = f32[3072,256]{0,1:T(8,128)S(1)} fusion(f32[256,1536]{1,0:T(8,128)S(1)} %convolution_add_fusion.1, f32[1,3072,1,1536]{1,3,2,0:T(8,128)} %copy.4), kind=kOutput, calls=%fused_computation.23 | convolution fusion | flops 7247757312 | bytes 23592960 | tf_op jit(solution)/shard_map/dot_general | solution.py:32
  421.5 3.1 pad_maximum_fusion.4
  429.2 11.7 %cholesky.282 = f32[128,128]{1,0:T(8,128)S(1)} custom-call(f32[128,128]{1,0:T(8,128)S(1)} %cholesky.352), custom_call_target="Cholesky" | custom-call | tf_op jit(solution)/shard_map/jit(cholesky)/cholesky | solution.py:25
  441.5 10.4 %custom-call.21 = f32[1,128,128]{1,2,0:T(8,128)} custom-call(f32[1,128,128]{2,1,0:T(8,128)S(1)} %get-tuple-element.99), custom_call_target="InvertDiagBlocksLowerTriangular" | custom-call | tf_op jit(solution)/shard_map/jit(cholesky)/cholesky | solution.py:25
  453.9 1.7 convolution_subtract_fusion.7
  455.6 13.2 %cholesky.299 = f32[128,128]{1,0:T(8,128)} custom-call(f32[128,128]{1,0:T(8,128)} %convolution_subtract_fusion.7), custom_call_target="Cholesky" | custom-call | tf_op jit(solution)/shard_map/jit(cholesky)/cholesky | solution.py:25
  474.0 5.3 while.10
  474.8 2.0 bitcast_dynamic-update-slice_fusion.10
  477.3 2.0 bitcast_dynamic-update-slice_fusion.10
  479.3 21.1 %custom-call.22 = f32[2,128,128]{1,2,0:T(8,128)} custom-call(f32[2,128,128]{2,1,0:T(8,128)} %get-tuple-element.40), custom_call_target="InvertDiagBlocksLowerTriangular" | custom-call | tf_op jit(solution)/shard_map/jit(_solve_triangular)/triangular_solve | solution.py:27
  504.2 5.0 all-reduce.18.cloned.1.call-done
  509.1 3.0 fusion.93
  512.1 1.5 fusion.94
  514.7 58.9 %reduce-scatter.2.cloned.1.call-done = f32[384,512]{0,1:T(8,128)} async-done(((f32[3072,512]{0,1:T(8,128)}), f32[384,512]{0,1:T(8,128)}) %reduce-scatter.2.cloned.1.call-update) | async-done | bytes 786448 | tf_op jit(solution)/shard_map/reduce_scatter | solution.py:73
  573.6 1.8 fusion.16
  575.4 1.8 fusion.18
  578.2 1.5 convolution_add_fusion.2
  580.4 11.7 %cholesky.316 = f32[128,128]{1,0:T(8,128)S(1)} custom-call(f32[128,128]{1,0:T(8,128)S(1)} %cholesky.355), custom_call_target="Cholesky" | custom-call | tf_op jit(solution)/shard_map/jit(cholesky)/cholesky | solution.py:25
  592.1 9.8 %custom-call.23 = f32[1,128,128]{1,2,0:T(8,128)S(1)} custom-call(f32[1,128,128]{2,1,0:T(8,128)S(1)} %get-tuple-element.95), custom_call_target="InvertDiagBlocksLowerTriangular" | custom-call | tf_op jit(solution)/shard_map/jit(cholesky)/cholesky | solution.py:25
  602.4 12.1 %cholesky.333 = f32[128,128]{1,0:T(8,128)S(1)} custom-call(f32[128,128]{1,0:T(8,128)S(1)} %convolution_subtract_fusion.6), custom_call_target="Cholesky" | custom-call | tf_op jit(solution)/shard_map/jit(cholesky)/cholesky | solution.py:25
  617.1 3.8 while.11
  617.7 1.3 bitcast_dynamic-update-slice_fusion.11
  619.6 1.3 bitcast_dynamic-update-slice_fusion.11
  620.9 19.7 %custom-call.24 = f32[2,128,128]{1,2,0:T(8,128)S(1)} custom-call(f32[2,128,128]{2,1,0:T(8,128)S(1)} %get-tuple-element.41), custom_call_target="InvertDiagBlocksLowerTriangular" | custom-call | tf_op jit(solution)/shard_map/jit(_solve_triangular)/triangular_solve | solution.py:27
  642.1 2.2 fusion.92
  644.4 1.4 fusion.20
  645.8 1.4 fusion.22
  647.2 1.5 convolution_subtract_fusion
  648.7 1.4 fusion.96
  650.2 1.5 convolution_subtract_fusion.1
  651.6 2.6 fusion.95
  654.2 24.6 %all-gather.2.cloned.1.call-done = f32[3072,512]{1,0:T(8,128)} async-done(((f32[384,512]{1,0:T(8,128)}), f32[3072,512]{1,0:T(8,128)}) %all-gather.2.cloned.1.call-update) | async-done | bytes 6291472 | tf_op jit(solution)/shard_map/all_gather | solution.py:84
  678.8 5.1 fusion.88
  683.9 20.7 %subtract_bitcast_fusion = f32[1,3072,1,1536]{1,3,2,0:T(8,128)} fusion(f32[3072,256]{1,0:T(8,128)S(1)} %copy-done.1, f32[3072,256]{1,0:T(8,128)S(1)} %get-tuple-element.87, f32[256,1536]{1,0:T(8,128)S(1)} %convolution_add_fusion.1, f32[256,1536]{1,0:T(8,128)S(1)} %copy-done.2, f32[1,3072,1,1536]{1,3,2,0:T(8,128)} %copy.4), kind=kOutput, calls=%fused_computation.14 | convolution fusion | flops 14502592512 | bytes 47185920 | tf_op jit(solution)/shard_map/dot_general | solution.py:32
  704.5 39.7 %copy.15 = f32[1,3072,1,1536]{3,2,1,0:T(1,128)} copy(f32[1,3072,1,1536]{1,3,2,0:T(8,128)} %subtract_bitcast_fusion) | data formatting | bytes 37748736
  744.2 24.4 %fusion.4 = f32[1,3072,1,1536]{3,1,2,0:T(8,128)} fusion(f32[1,3072,1,1536]{3,2,1,0:T(1,128)} %param.6, f32[3072,256]{1,0:T(8,128)} %copy-done, f32[3072,256]{1,0:T(8,128)} %get-tuple-element.86, f32[256,1536]{1,0:T(8,128)S(1)} %convolution_add_fusion.1, f32[256,1536]{1,0:T(8,128)S(1)} %fusion.96), kind=kOutput, calls=%fused_computation.13 | convolution fusion | flops 14502592512 | bytes 47185920 | tf_op jit(solution)/shard_map/dot_general | solution.py:32
  768.6 22.3 %copy.16 = f32[1,3072,1,1536]{3,2,1,0:T(1,128)} copy(f32[1,3072,1,1536]{3,1,2,0:T(8,128)} %fusion.4) | data formatting | bytes 37748736
  (143 shorter events, 48.5 us)
Async XLA Ops:
  7.2 1.4 slice-start
  7.2 186.2 %all-reduce.10.cloned.1.call-start = ((), (), s32[]{:S(2)}) async-start(), calls=%async_computation.1 | async-start | bytes 2097152 | tf_op jit(solution)/shard_map/psum | solution.py:59
  59.9 270.8 %all-reduce.12.cloned.1.call-start = ((), (), s32[]{:S(2)}) async-start(), calls=%async_computation.2 | async-start | bytes 6291456 | tf_op jit(solution)/shard_map/psum | solution.py:11
  197.3 1.2 copy-start.7
  197.3 154.9 %all-reduce.14.cloned.1.call-start = ((), (), s32[]{:S(2)}) async-start(), calls=%async_computation.3 | async-start | bytes 3145728 | tf_op jit(solution)/shard_map/psum | solution.py:11
  201.2 0.7 copy-start.14
  284.4 46.3 %copy-start.11 = (f32[256,256]{1,0:T(8,128)}, f32[256,256]{1,0:T(8,128)S(1)}, u32[]{:S(2)}) copy-start(f32[256,256]{1,0:T(8,128)S(1)} %get-tuple-element.325) | copy-start | bytes 786436
  284.5 224.7 %all-reduce.18.cloned.1.call-start = ((), (), s32[]{:S(2)}) async-start(), calls=%async_computation.7 | async-start | bytes 6291456 | tf_op jit(solution)/shard_map/psum | solution.py:70
  308.5 20.7 %copy-start.16 = (f32[2,128,128]{1,2,0:T(8,128)}, f32[2,128,128]{1,2,0:T(8,128)S(1)}, u32[]{:S(2)}) copy-start(f32[2,128,128]{1,2,0:T(8,128)S(1)} %custom-call.20) | copy-start | bytes 393220
  337.7 32.0 %copy-start = (f32[3072,256]{1,0:T(8,128)}, f32[3072,256]{1,0:T(8,128)S(1)}, u32[]{:S(2)}) copy-start(f32[3072,256]{1,0:T(8,128)S(1)} %convolution_add_fusion) | copy-start | bytes 9437188
  388.9 0.9 copy-start.10
  388.9 2.0 copy-start.17
  388.9 184.7 %reduce-scatter.2.cloned.1.call-start = ((), (), s32[]{:S(2)}) async-start(), calls=%async_computation.4 | async-start | bytes 7077888 | tf_op jit(solution)/shard_map/reduce_scatter | solution.py:73
  424.6 1.2 copy-start.8
  424.6 219.8 %all-reduce.16.cloned.1.call-start = ((), (), s32[]{:S(2)}) async-start(), calls=%async_computation.6 | async-start | bytes 1048576 | tf_op jit(solution)/shard_map/psum | solution.py:85
  428.5 0.7 copy-start.13
  440.9 0.6 copy-start.15
  470.4 1.9 copy-start.12
  509.1 3.0 copy-start.4
  514.5 164.3 %all-gather.2.cloned.1.call-start = ((), (), s32[]{:S(2)}) async-start(), calls=%async_computation.5 | async-start | bytes 7077888 | tf_op jit(solution)/shard_map/all_gather | solution.py:84
  579.7 61.2 %copy-start.6 = (f32[256,256]{1,0:T(8,128)}, f32[256,256]{1,0:T(8,128)S(1)}, u32[]{:S(2)}) copy-start(f32[256,256]{1,0:T(8,128)S(1)} %convolution_add_fusion.2) | copy-start | bytes 786436
  641.2 6.0 copy-start.5
  644.4 4.3 copy-start.9
  647.2 3.0 copy-start.3
  678.8 5.1 copy-start.1
  678.8 5.1 copy-start.2
Sparse Core Ops, SparseCore 0:
  60.0 133.3 all-reduce.9
  197.4 68.5 all-reduce.11
  284.6 67.5 all-reduce.13
  389.1 120.0 all-reduce.17
  512.9 60.6 reduce-scatter.1
  576.6 55.6 all-reduce.15
  634.2 44.5 all-gather.1
where the time goes:
time: 807 us; the launch traced here: 798 us
  other arithmetic  237 us (29%)
  waiting for transfers between devices  233 us (29%)
  matrix products  167 us (21%)
  local copies, waits for them, and re-layouts  140 us (17%)
  between operations  19.9 us (2%)
    psum x1, waiting for transfers between devices, on_device(): small = lax.psum(small, ('row', 'col'))  130 us
    dot_general x6, matrix products, fast_matmul(): jnp.dot(left, right, precision=lax.Precision.HIGH, preferred_element_type...  109 us
    unnamed x40, local copies, waits for them, and re-layouts  108 us
    another operation x14, other arithmetic, general_inverse(): lower = jnp.linalg.cholesky(matmul(square, square.T))  72.6 us
    another operation x14, other arithmetic, inverse_factor(): lower = jnp.linalg.cholesky(gram)  69.4 us
    reduce_scatter x1, waiting for transfers between devices, on_device(): lax.psum_scatter(jnp.concatenate([fast_matmul(amat, vectors_t.T), fast_ma...  58.9 us
    dot_general x22, matrix products, matmul(): jnp.dot(left, right, precision=lax.Precision.HIGHEST, preferred_element_t...  42.6 us
    another operation x4, other arithmetic, general_inverse(): linv = jax.scipy.linalg.solve_triangular(lower, ident, lower=True)  41.8 us
  transfers between devices with their start and end apart: 7, of which 5 were waited for; matrix products, arithmetic and copies ran while one was open for 42% of the time, Pallas kernels for 0%

commit v1 on v0

v1 whole, which is shorter than its diff:
```python
import functools
import jax
import jax.numpy as jnp
from jax import lax
from jax.experimental import pallas as pl
from jax.experimental.pallas import tpu as pltpu
from jax.sharding import PartitionSpec as P

NB = 256
LANES = 128
SUB = 8
F32 = jnp.float32
BF16 = jnp.bfloat16
MIB = 1 << 20


def matmul(left, right):
    return jnp.dot(left, right, precision=lax.Precision.HIGHEST, preferred_element_type=F32)


def split(x):
    hi = x.astype(BF16)
    return hi, (x - hi.astype(F32)).astype(BF16)


def split_out(x):
    hi = lax.reduce_precision(x, 8, 7)
    return hi.astype(BF16), (x - hi).astype(BF16)


def dot_t(left, right, dims):
    return lax.dot_general(left, right, (dims, ((), ())), preferred_element_type=F32)


def dot3(left, right, dims=((1,), (0,))):
    lh, ll = left
    rh, rl = right
    return dot_t(lh, rh, dims) + (dot_t(lh, rl, dims) + dot_t(ll, rh, dims))


def load_cols(ref, first, count, rows, per_row):
    parts = [ref[pl.ds(first + k, rows, stride=per_row), :] for k in range(count)]
    return jnp.concatenate(parts, axis=1)


def left_products_kernel(rows_blk, per_row, pt_ref, raw_ref, out_ref):
    step = pl.program_id(0)

    @pl.when(step == 0)
    def _():
        out_ref[...] = jnp.zeros_like(out_ref)

    pt = split(pt_ref[...])
    group = 2
    for first in range(0, per_row, group):
        block = split(load_cols(raw_ref, first, group, rows_blk, per_row))
        cols = pl.ds(first * LANES, group * LANES)
        out_ref[:, cols] += dot3(pt, block)


def left_products(panel_t, raw, rows, cols, rows_blk):
    width = panel_t.shape[0]
    per_row = cols // LANES
    return pl.pallas_call(
        functools.partial(left_products_kernel, rows_blk, per_row),
        grid=(rows // rows_blk,),
        out_shape=jax.ShapeDtypeStruct((width, cols), F32),
        in_specs=[
            pl.BlockSpec((width, rows_blk), lambda i: (0, i)),
            pl.BlockSpec((rows_blk * per_row, LANES), lambda i: (i, 0)),
        ],
        out_specs=pl.BlockSpec((width, cols), lambda i: (0, 0)),
        compiler_params=pltpu.CompilerParams(vmem_limit_bytes=48 * MIB),
        cost_estimate=pl.CostEstimate(
            flops=6 * width * rows * cols, bytes_accessed=4 * rows * cols, transcendentals=0
        ),
        name="left_products",
    )(panel_t, raw)


def right_products_kernel(rows_blk, per_row, whi_ref, wlo_ref, a_ref, b_ref, out_ref):
    width = whi_ref.shape[1]
    group = 2
    for side, raw_ref in enumerate((a_ref, b_ref)):
        total = None
        for first in range(0, per_row, group):
            block = split(load_cols(raw_ref, first, group, rows_blk, per_row))
            rows = pl.ds(first * LANES, group * LANES)
            term = dot3(block, (whi_ref[rows, :], wlo_ref[rows, :]))
            total = term if total is None else total + term
        out_ref[:, side * width : (side + 1) * width] = total


def right_products(wt, raw_a, raw_b, rows, cols, rows_blk):
    width = wt.shape[1]
    per_row = cols // LANES
    raw_spec = pl.BlockSpec((rows_blk * per_row, LANES), lambda i: (i, 0))
    wide = pl.BlockSpec((cols, width), lambda i: (0, 0))
    whi, wlo = split_out(wt)
    return pl.pallas_call(
        functools.partial(right_products_kernel, rows_blk, per_row),
        grid=(rows // rows_blk,),
        out_shape=jax.ShapeDtypeStruct((rows, 2 * width), F32),
        in_specs=[wide, wide, raw_spec, raw_spec],
        out_specs=pl.BlockSpec((rows_blk, 2 * width), lambda i: (i, 0)),
        compiler_params=pltpu.CompilerParams(vmem_limit_bytes=48 * MIB),
        cost_estimate=pl.CostEstimate(
            flops=12 * width * rows * cols, bytes_accessed=8 * rows * cols, transcendentals=0
        ),
        name="right_products",
    )(whi, wlo, raw_a, raw_b)


def update_kernel(rows_blk, per_row, v_ref, s_ref, dhi_ref, dlo_ref, raw_ref, out_ref):
    width = v_ref.shape[1]
    left = (split(v_ref[...]), split(s_ref[...]))
    group = 2
    for first in range(0, per_row, group):
        cols = pl.ds(first * LANES, group * LANES)
        total = None
        for part in range(2):
            rows = pl.ds(part * width, width)
            term = dot3(left[part], (dhi_ref[rows, cols], dlo_ref[rows, cols]))
            total = term if total is None else total + term
        for k in range(group):
            where = pl.ds(first + k, rows_blk, stride=per_row)
            out_ref[where, :] = raw_ref[where, :] - total[:, k * LANES : (k + 1) * LANES]


def update(vectors, mixed, side, low, raw, rows, cols, rows_blk):
    width = vectors.shape[1]
    per_row = cols // LANES
    raw_spec = pl.BlockSpec((rows_blk * per_row, LANES), lambda i: (i, 0))
    low_spec = pl.BlockSpec((2 * width, cols), lambda i: (0, 0))
    dhi, dlo = split_out(low)
    return pl.pallas_call(
        functools.partial(update_kernel, rows_blk, per_row),
        grid=(rows // rows_blk,),
        out_shape=jax.ShapeDtypeStruct((rows * per_row, LANES), F32),
        in_specs=[
            pl.BlockSpec((rows_blk, width), lambda i: (i, 0)),
            pl.BlockSpec((rows_blk, width), lambda i, side=side: (i, side)),
            low_spec,
            low_spec,
            raw_spec,
        ],
        out_specs=raw_spec,
        compiler_params=pltpu.CompilerParams(vmem_limit_bytes=48 * MIB),
        cost_estimate=pl.CostEstimate(
            flops=12 * width * rows * cols, bytes_accessed=8 * rows * cols, transcendentals=0
        ),
        name="update",
    )(vectors, mixed, dhi, dlo, raw)


def iota(shape, dim):
    return lax.broadcasted_iota(jnp.int32, shape, dim)


def pick_lane(rows, lane):
    hit = iota(rows.shape, 1) == lane
    col = jnp.sum(jnp.where(hit, rows, 0.0), axis=1, keepdims=True)
    return jnp.broadcast_to(col, (rows.shape[0], LANES))


def spread(x, row, width):
    return jnp.broadcast_to(x[row : row + 1, :], (x.shape[0], width))


def widen(x, width):
    return jnp.concatenate([x] * (width // LANES), axis=1)


def cholesky_panel(rows, first):
    count, width = rows.shape
    ri = iota((count, LANES), 0)
    cols = [pick_lane(rows, first + t) for t in range(count)]
    for s in range(count):
        pivot = spread(cols[s], s, LANES)
        root = lax.rsqrt(pivot)
        root = root * (1.5 - 0.5 * pivot * root * root)
        factor = cols[s] * root
        below = jnp.where(ri > s, factor, 0.0)
        row = spread(rows, s, width) * widen(root, width)
        here = iota((count, width), 0) == s
        rows = jnp.where(here, row, rows - widen(below, width) * row)
        for t in range(s + 1, count):
            cols[t] = cols[t] - below * spread(factor, t, LANES)
    return rows


def inverse_panel(rows, first):
    count, width = rows.shape
    ri = iota((count, LANES), 0)
    cols = [pick_lane(rows, first + t) for t in range(count)]
    lane = iota((count, width), 1)
    sub = iota((count, width), 0)
    inside = (lane >= first) & (lane < first + count)
    rows = jnp.where(inside, jnp.where(lane - first == sub, 1.0, 0.0), rows)
    for s in range(count):
        recip = 1.0 / spread(cols[s], s, LANES)
        others = jnp.where(ri == s, 0.0, cols[s])
        row = spread(rows, s, width) * widen(recip, width)
        rows = jnp.where(sub == s, row, rows - widen(others, width) * row)
        for t in range(s + 1, count):
            turn = spread(cols[t], s, LANES) * recip
            cols[t] = jnp.where(ri == s, turn, cols[t] - others * turn)
    return rows


def outer(left, right):
    return lax.dot_general(
        left, right, (((0,), (0,)), ((), ())), precision=lax.Precision.HIGHEST, preferred_element_type=F32
    )


def cholesky_kernel(gram_ref, lower_ref, rest, upper):
    n = gram_ref.shape[1]
    step = 16
    rest[...] = gram_ref[...]

    def body(p, carry):
        first = pl.multiple_of(p * step, step)
        rows = pl.ds(first, step)
        done = [cholesky_panel(rest[k, rows, :], first) for k in range(2)]
        for k in range(2):
            upper[k, rows, :] = done[k]
            rest[k] -= outer(done[k], done[k])
        return carry

    lax.fori_loop(0, n // step, body, 0)
    keep = iota((n, n), 0) >= iota((n, n), 1)
    for k in range(2):
        lower_ref[k] = jnp.where(keep, upper[k].T, 0.0)


def cholesky_pair(gram):
    return pl.pallas_call(
        cholesky_kernel,
        out_shape=jax.ShapeDtypeStruct(gram.shape, F32),
        in_specs=[pl.BlockSpec(memory_space=pltpu.VMEM)],
        out_specs=pl.BlockSpec(memory_space=pltpu.VMEM),
        scratch_shapes=[pltpu.VMEM(gram.shape, F32)] * 2,
        cost_estimate=pl.CostEstimate(flops=10**8, bytes_accessed=10**6, transcendentals=0),
        name="cholesky_pair",
    )(gram)


def inverse_kernel(step, gram_ref, lower_ref, block_ref, out_ref, mat, mat_t):
    n = gram_ref.shape[1]
    left = gram_ref[0] + matmul(lower_ref[0], block_ref[0])
    right = gram_ref[1] + matmul(block_ref[1], lower_ref[1].T)
    mat[0] = left
    mat_t[0] = left.T
    mat[1] = right
    mat_t[1] = right.T

    def body(p, carry):
        first = pl.multiple_of(p * step, step)
        rows = pl.ds(first, step)
        lane = iota((step, n), 1)
        sub = iota((step, n), 0)
        inside = (lane >= first) & (lane < first + step)
        minus = jnp.where(lane - first == sub, -1.0, 0.0)
        wide = [inverse_panel(mat[k, rows, :], first) for k in range(2)]
        tall = [jnp.where(inside, minus, mat_t[k, rows, :]) for k in range(2)]
        ri = iota((n, n), 0)
        ci = iota((n, n), 1)
        clear = ((ri >= first) & (ri < first + step)) | ((ci >= first) & (ci < first + step))
        for k in range(2):
            mat[k] = jnp.where(clear, 0.0, mat[k]) - outer(tall[k], wide[k])
            mat_t[k] = jnp.where(clear, 0.0, mat_t[k]) - outer(wide[k], tall[k])
        return carry

    lax.fori_loop(0, n // step, body, 0)
    out_ref[...] = mat[...]


def inverse_pair(gram, lower, block):
    return pl.pallas_call(
        functools.partial(inverse_kernel, 16),
        out_shape=jax.ShapeDtypeStruct(gram.shape, F32),
        in_specs=[pl.BlockSpec(memory_space=pltpu.VMEM)] * 3,
        out_specs=pl.BlockSpec(memory_space=pltpu.VMEM),
        scratch_shapes=[pltpu.VMEM(gram.shape, F32)] * 2,
        cost_estimate=pl.CostEstimate(flops=10**8, bytes_accessed=10**6, transcendentals=0),
        name="inverse_pair",
    )(gram, lower, block)


MESH = pl.DeviceIdType.MESH
VMEM_SPEC = pl.BlockSpec(memory_space=pltpu.VMEM)
ANY_SPEC = pl.BlockSpec(memory_space=pl.ANY)
DMA = pltpu.SemaphoreType.DMA


def remote(src, dst, send_sem, recv_sem, row, col):
    return pltpu.make_async_remote_copy(
        src_ref=src, dst_ref=dst, send_sem=send_sem, recv_sem=recv_sem, device_id=(row, col), device_id_type=MESH
    )


def bit(x, k):
    return lax.rem(lax.div(x, 2**k), 2)


def log2(n):
    assert n & (n - 1) == 0
    return n.bit_length() - 1


def ring_place(x, n):
    above, place = 0, 0
    for k in reversed(range(log2(n))):
        above = lax.rem(above + bit(x, k), 2)
        place = place + above * 2**k
    return place


def ring_device(place, n):
    x = 0
    for k in range(log2(n)):
        x = x + lax.rem(bit(place, k) + bit(place, k + 1), 2) * 2**k
    return x


def greet(peers, count):
    barrier = pltpu.get_barrier_semaphore()

    def hello(row, col):
        pl.semaphore_signal(barrier, inc=1, device_id=(row, col), device_id_type=MESH)

    for when, row, col in peers:
        if when is None:
            hello(row, col)
        else:
            pl.when(when)(functools.partial(hello, row, col))
    pl.semaphore_wait(barrier, count)


def params(collective_id, vmem=48 * MIB):
    return pltpu.CompilerParams(collective_id=collective_id, has_side_effects=True, vmem_limit_bytes=vmem)


def cross_peers(n_row, n_col, row, col):
    return [(row != r, r, col) for r in range(n_row)] + [(col != c, row, c) for c in range(n_col)]


def broadcast_kernel(n_row, n_col, chunks, panel_in, strip_in, panel_out, strip_out, panel, strip, local, send, recv):
    row, col = lax.axis_index("row"), lax.axis_index("col")
    rows, width = panel.shape[0], strip.shape[0]
    place = ring_place(col, n_col)
    ahead = ring_device(lax.rem(place + 1, n_col), n_col)
    behind = ring_device(lax.rem(place + n_col - 1, n_col), n_col)
    greet(
        [
            (None, row, ahead),
            (None, row, behind),
            (row > 0, row - 1, col),
            (row < n_row - 1, row + 1, col),
        ],
        2 + lax.min(row, 1) + lax.min(n_row - 1 - row, 1),
    )

    @pl.when(place == 0)
    def _():
        load = pltpu.make_async_copy(panel_in, panel, local.at[0])
        load.start()
        load.wait()

    @pl.when(row == n_row - 1)
    def _():
        load = pltpu.make_async_copy(strip_in, strip, local.at[1])
        load.start()
        load.wait()

    half, part, piece = rows // 2, rows // 2 // chunks, width // chunks
    back = lax.rem(n_col - place, n_col)
    streams = (
        (panel, 0, part, place, place > 0, place < n_col - 1, row, ahead),
        (panel, half, part, back, place > 0, place != 1, row, behind),
        (strip, 0, piece, n_row - 1 - row, row < n_row - 1, row > 0, row - 1, col),
    )

    def copy(k, i):
        buf, base, size, _, _, _, to_row, to_col = streams[k]
        where = pl.ds(pl.multiple_of(base + i * size, SUB), size)
        return remote(buf.at[where], buf.at[where], send.at[k, i], recv.at[k, i], to_row, to_col)

    def turn(t, carry):
        for k, (_, _, _, late, gets, gives, _, _) in enumerate(streams):
            i = t - late

            @pl.when((i >= 0) & (i < chunks))
            def _():
                pl.when(gets)(lambda: copy(k, i).wait_recv())
                pl.when(gives)(lambda: copy(k, i).start())

        return carry

    lax.fori_loop(0, chunks + max(n_col, n_row) - 1, turn, 0)
    stores = [
        pltpu.make_async_copy(panel, panel_out, local.at[2]),
        pltpu.make_async_copy(strip, strip_out, local.at[3]),
    ]
    for store in stores:
        store.start()

    def finish(i, carry):
        for k, (_, _, _, _, _, gives, _, _) in enumerate(streams):
            pl.when(gives)(lambda: copy(k, i).wait_send())
        return carry

    lax.fori_loop(0, chunks, finish, 0)
    for store in stores:
        store.wait()


def broadcast_pair(panel, strip, n_row, n_col, collective_id, chunks=8):
    return pl.pallas_call(
        functools.partial(broadcast_kernel, n_row, n_col, chunks),
        out_shape=(
            jax.ShapeDtypeStruct(panel.shape, F32),
            jax.ShapeDtypeStruct(strip.shape, F32),
        ),
        in_specs=[ANY_SPEC] * 2,
        out_specs=(ANY_SPEC, ANY_SPEC),
        scratch_shapes=[
            pltpu.VMEM(panel.shape, F32),
            pltpu.VMEM(strip.shape, F32),
            DMA((4,)),
            DMA((3, chunks)),
            DMA((3, chunks)),
        ],
        compiler_params=params(collective_id),
        cost_estimate=pl.CostEstimate(flops=10**10, bytes_accessed=10**7, transcendentals=0),
        name="broadcast_pair",
    )(panel, strip)


def grams_kernel(
    n_row, n_col, g1, pt, g2, ce, gram_out, block_out,
    part1, part2, left, right, send1, send2, sends, recv1, recv2, recvs, recv_l, recv_r,
):
    row, col = lax.axis_index("row"), lax.axis_index("col")
    width = g1.shape[0]
    qr, qc = width // n_row, width // n_col
    end_row, end_col = n_row - 1, n_col - 1
    greet(cross_peers(n_row, n_col, row, col), n_row + n_col - 2)
    source1, source2 = col == 0, row == end_row

    def first_left(r):
        return remote(g1.at[pl.ds(r * qr, qr)], part1.at[row], send1.at[0, r], recv1.at[row], r, 0)

    def first_top(r):
        return remote(pt.at[pl.ds(r * qr, qr)], left.at[r, 1], send1.at[1, r], recvs.at[0], r, 0)

    def first_right(c):
        return remote(g2.at[pl.ds(c * qc, qc)], part2.at[col], send2.at[0, c], recv2.at[col], end_row, c)

    def first_end(c):
        return remote(ce.at[pl.ds(c * qc, qc)], right.at[c, 1], send2.at[1, c], recvs.at[1], end_row, c)

    def to_col(c):
        return remote(left.at[row], left.at[row], sends.at[0, c], recv_l.at[row], row, c)

    def to_row(r):
        return remote(right.at[col], right.at[col], sends.at[1, r], recv_r.at[col], r, col)

    def spread_left(r):
        return remote(left.at[row], left.at[row], sends.at[2, r], recv_l.at[row], r, col)

    def spread_right(c):
        return remote(right.at[col], right.at[col], sends.at[3, c], recv_r.at[col], row, c)

    def each(count, skip, when, action):
        for k in range(count):
            pl.when(when & (skip != k))(functools.partial(action, k))

    always = row >= 0
    each(n_row, row, source1, lambda r: first_left(r).start())
    each(n_col, col, source2, lambda c: first_right(c).start())
    each(n_row, row, source1 & (row == 0), lambda r: first_top(r).start())
    each(n_col, col, source2 & (col == end_col), lambda c: first_end(c).start())

    @pl.when(source1)
    def _():
        mine = pl.ds(pl.multiple_of(row * qr, SUB), qr)
        part1[row] = g1[mine, :]

        @pl.when(row == 0)
        def _():
            left[0, 1] = pt[0:qr, :]

        for r in range(n_row):
            pl.when(row != r)(
                lambda: remote(part1.at[r], part1.at[r], send1.at[0, r], recv1.at[r], r, 0).wait_recv()
            )
        pl.when(row != 0)(lambda: remote(left.at[row, 1], left.at[row, 1], send1.at[1, 0], recvs.at[0], 0, 0).wait_recv())
        total = part1[0]
        for r in range(1, n_row):
            total = total + part1[r]
        left[row, 0] = total

    each(n_col, 0, source1, lambda c: to_col(c).start())

    @pl.when(source2)
    def _():
        mine = pl.ds(pl.multiple_of(col * qc, SUB), qc)
        part2[col] = g2[mine, :]

        @pl.when(col == end_col)
        def _():
            right[end_col, 1] = ce[end_col * qc : (end_col + 1) * qc, :]

        for c in range(n_col):
            pl.when(col != c)(
                lambda: remote(part2.at[c], part2.at[c], send2.at[0, c], recv2.at[c], end_row, c).wait_recv()
            )
        pl.when(col != end_col)(
            lambda: remote(right.at[col, 1], right.at[col, 1], send2.at[1, 0], recvs.at[1], end_row, 0).wait_recv()
        )
        total = part2[0]
        for c in range(1, n_col):
            total = total + part2[c]
        right[col, 0] = total

    each(n_row, end_row, source2, lambda r: to_row(r).start())

    def got_left(r):
        remote(left.at[r], left.at[r], sends.at[0, 0], recv_l.at[r], row, 0).wait_recv()

    def got_right(c):
        remote(right.at[c], right.at[c], sends.at[1, 0], recv_r.at[c], 0, col).wait_recv()

    pl.when(col != 0)(lambda: got_left(row))
    each(n_row, row, always, lambda r: spread_left(r).start())
    pl.when(row != end_row)(lambda: got_right(col))
    each(n_col, col, always, lambda c: spread_right(c).start())
    each(n_row, row, always, got_left)
    each(n_col, col, always, got_right)
    for r in range(n_row):
        gram_out[0, r * qr : (r + 1) * qr, :] = left[r, 0]
        block_out[0, r * qr : (r + 1) * qr, :] = left[r, 1]
    for c in range(n_col):
        gram_out[1, c * qc : (c + 1) * qc, :] = right[c, 0]
        block_out[1, c * qc : (c + 1) * qc, :] = right[c, 1]
    each(n_row, row, source1, lambda r: first_left(r).wait_send())
    each(n_col, col, source2, lambda c: first_right(c).wait_send())
    each(n_row, row, source1 & (row == 0), lambda r: first_top(r).wait_send())
    each(n_col, col, source2 & (col == end_col), lambda c: first_end(c).wait_send())
    each(n_col, 0, source1, lambda c: to_col(c).wait_send())
    each(n_row, end_row, source2, lambda r: to_row(r).wait_send())
    each(n_row, row, always, lambda r: spread_left(r).wait_send())
    each(n_col, col, always, lambda c: spread_right(c).wait_send())


def share_grams(g1, pt, g2, ce, n_row, n_col, collective_id):
    width = g1.shape[0]
    most = max(n_row, n_col)
    pair = jax.ShapeDtypeStruct((2, width, width), F32)
    return pl.pallas_call(
        functools.partial(grams_kernel, n_row, n_col),
        out_shape=(pair, pair),
        in_specs=[VMEM_SPEC] * 4,
        out_specs=(VMEM_SPEC, VMEM_SPEC),
        scratch_shapes=[
            pltpu.VMEM((n_row, width // n_row, width), F32),
            pltpu.VMEM((n_col, width // n_col, width), F32),
            pltpu.VMEM((n_row, 2, width // n_row, width), F32),
            pltpu.VMEM((n_col, 2, width // n_col, width), F32),
            DMA((2, n_row)),
            DMA((2, n_col)),
            DMA((4, most)),
            DMA((n_row,)),
            DMA((n_col,)),
            DMA((2,)),
            DMA((n_row,)),
            DMA((n_col,)),
        ],
        compiler_params=params(collective_id),
        cost_estimate=pl.CostEstimate(flops=5 * 10**9, bytes_accessed=10**6, transcendentals=0),
        name="share_grams",
    )(g1, pt, g2, ce)


def cross_kernel(n_row, n_col, mine, out, parts, rows, send_r, send_c, recv_r, recv_c):
    row, col = lax.axis_index("row"), lax.axis_index("col")
    count = mine.shape[0]
    greet(cross_peers(n_row, n_col, row, col), n_row + n_col - 2)

    def over_row(r, slot):
        return remote(mine, parts.at[slot], send_r.at[r], recv_r.at[slot], r, col)

    def over_col(c, slot):
        return remote(rows.at[slot], rows.at[slot], send_c.at[c], recv_c.at[slot], row, c)

    for r in range(n_row):
        pl.when(row != r)(lambda: over_row(r, row).start())
    parts[row] = mine[...]
    for r in range(n_row):
        pl.when(row != r)(lambda: over_row(r, r).wait_recv())
    total = parts[0]
    for r in range(1, n_row):
        total = total + parts[r]
    rows[col] = total
    for c in range(n_col):
        pl.when(col != c)(lambda: over_col(c, col).start())
    for c in range(n_col):
        pl.when(col != c)(lambda: over_col(c, c).wait_recv())
    for c in range(n_col):
        out[c * count : (c + 1) * count, :] = rows[c]
    for r in range(n_row):
        pl.when(row != r)(lambda: over_row(r, row).wait_send())
    for c in range(n_col):
        pl.when(col != c)(lambda: over_col(c, col).wait_send())


def sum_cross(part, n_row, n_col, collective_id):
    count, width = part.shape
    return pl.pallas_call(
        functools.partial(cross_kernel, n_row, n_col),
        out_shape=jax.ShapeDtypeStruct((n_col * count, width), F32),
        in_specs=[VMEM_SPEC],
        out_specs=VMEM_SPEC,
        scratch_shapes=[
            pltpu.VMEM((n_row, count, width), F32),
            pltpu.VMEM((n_col, count, width), F32),
            DMA((n_row,)),
            DMA((n_col,)),
            DMA((n_row,)),
            DMA((n_col,)),
        ],
        compiler_params=params(collective_id),
        cost_estimate=pl.CostEstimate(flops=5 * 10**9, bytes_accessed=10**6, transcendentals=0),
        name="sum_cross",
    )(part)


def sum_col_kernel(n_col, part, out, acc, inbox, full, local, send, recv):
    row, col = lax.axis_index("row"), lax.axis_index("col")
    rows = acc.shape[0]
    levels = log2(n_col)
    half = rows // 2
    orders = (list(range(levels)), [0] + list(reversed(range(1, levels))))
    loads = [
        pltpu.make_async_copy(part.at[pl.ds(g * half, half)], acc.at[pl.ds(g * half, half)], local.at[g])
        for g in range(2)
    ]
    for load in loads:
        load.start()
    bits = [bit(col, k) for k in range(levels)]
    partner = [col + (1 - 2 * bits[k]) * 2**k for k in range(levels)]
    greet([(None, row, partner[k]) for k in range(levels)], levels)
    start = [g * half for g in range(2)]
    block = 16
    for load in loads:
        load.wait()

    def reduce_copy(g, j):
        k, size = orders[g][j], half >> (j + 1)
        away = pl.ds(pl.multiple_of(start[g] + (1 - bits[k]) * size, SUB), size)
        slot = pl.ds(half - (half >> j), size)
        return remote(acc.at[away], inbox.at[g, slot], send.at[g, j], recv.at[g, j], row, partner[k])

    sent = []
    for j in range(levels):
        copies = [reduce_copy(g, j) for g in range(2)]
        for copy in copies:
            copy.start()
        sent += copies
        for g in range(2):
            k, size = orders[g][j], half >> (j + 1)
            copies[g].wait_recv()
            kept = start[g] + bits[k] * size
            slot = half - (half >> j)

            goal = full if j == levels - 1 else acc

            def add(i, carry, kept=kept, slot=slot, g=g, goal=goal):
                here = pl.ds(pl.multiple_of(kept + i * block, SUB), block)
                goal[here, :] = acc[here, :] + inbox[g, pl.ds(pl.multiple_of(slot + i * block, SUB), block), :]
                return carry

            lax.fori_loop(0, size // block, add, 0)
            start[g] = kept
    for j in reversed(range(levels)):
        copies = []
        for g in range(2):
            k, size = orders[g][j], half >> (j + 1)
            here = pl.ds(pl.multiple_of(start[g], SUB), size)
            there = pl.ds(pl.multiple_of(start[g] + (1 - 2 * bits[k]) * size, SUB), size)
            slot = levels + j
            out_copy = remote(full.at[here], full.at[here], send.at[g, slot], recv.at[g, slot], row, partner[k])
            in_copy = remote(full.at[there], full.at[there], send.at[g, slot], recv.at[g, slot], row, partner[k])
            copies.append((out_copy, in_copy))
            out_copy.start()
        for g in range(2):
            k, size = orders[g][j], half >> (j + 1)
            copies[g][1].wait_recv()
            start[g] = start[g] - bits[k] * size
            sent.append(copies[g][0])
    store = pltpu.make_async_copy(full, out, local.at[2])
    store.start()
    for copy in sent:
        copy.wait_send()
    store.wait()


def sum_col(part, n_col, collective_id):
    rows, width = part.shape
    levels = log2(n_col)
    half = rows // 2
    return pl.pallas_call(
        functools.partial(sum_col_kernel, n_col),
        out_shape=jax.ShapeDtypeStruct(part.shape, F32),
        in_specs=[ANY_SPEC],
        out_specs=ANY_SPEC,
        scratch_shapes=[
            pltpu.VMEM(part.shape, F32),
            pltpu.VMEM((2, half - half // n_col, width), F32),
            pltpu.VMEM(part.shape, F32),
            DMA((3,)),
            DMA((2, 2 * levels)),
            DMA((2, 2 * levels)),
        ],
        compiler_params=params(collective_id),
        cost_estimate=pl.CostEstimate(flops=2 * 10**10, bytes_accessed=10**7, transcendentals=0),
        name="sum_col",
    )(part)


def on_device(n_row, n_col, pencil_a, pencil_b):
    rows, cols = pencil_a.shape[1], pencil_a.shape[3]
    width = NB
    row, col = lax.axis_index("row"), lax.axis_index("col")
    raw_a = pencil_a.reshape(rows * cols // LANES, LANES)
    raw_b = pencil_b.reshape(rows * cols // LANES, LANES)
    rows_blk = rows // 4
    own_panel = pencil_a[0, :, 0, :width]
    own_strip = pencil_b[0, rows - width :, 0, :]
    gram, block = share_grams(
        matmul(own_panel.T, own_panel),
        own_panel[:width],
        matmul(own_strip, own_strip.T),
        own_strip[:, cols - width :],
        n_row,
        n_col,
        0,
    )
    panel, strip = broadcast_pair(own_panel, own_strip, n_row, n_col, 1)
    lower = cholesky_pair(gram)
    top = jnp.where(row == 0, lower[0].T, 0.0)
    end = jnp.where(col == n_col - 1, lower[1], 0.0)
    vectors = panel + jnp.pad(top, ((0, rows - width), (0, 0)))
    vectors_t = strip + jnp.pad(end, ((0, 0), (cols - width, 0)))
    flipped = vectors.T
    products = [left_products(flipped, raw, rows, cols, rows_blk) for raw in (raw_a, raw_b)]
    products = lax.psum(products, "row")
    inverse = inverse_pair(gram, lower, block)
    mixed = sum_col(right_products(vectors_t.T, raw_a, raw_b, rows, cols, rows_blk), n_col, 2)
    slim = width // n_col
    mine = lax.dynamic_slice(flipped, (col * slim, 0), (slim, rows))
    crossed = sum_cross(jnp.dot(mine, mixed, precision=lax.Precision.HIGH, preferred_element_type=F32), n_row, n_col, 3)
    turned = matmul(inverse[1], vectors_t)
    outs = []
    for side, raw in enumerate((raw_a, raw_b)):
        inner = products[side] - matmul(crossed[:, side * width : (side + 1) * width], turned)
        low = jnp.concatenate([matmul(inverse[0], inner), turned], axis=0)
        outs.append(update(vectors, mixed, side, low, raw, rows, cols, rows_blk))
    return tuple(out.reshape(1, rows, 1, cols) for out in outs)


def solution(mesh):
    placed = (P("row", None, "col", None), P("row", None, "col", None))
    return jax.shard_map(
        functools.partial(on_device, mesh.shape["row"], mesh.shape["col"]),
        mesh=mesh,
        in_specs=placed,
        out_specs=placed,
        check_vma=False,
    )
```

time: 807 us -> 375 us (0.46)
  Pallas kernels: 0 us -> 312 us
  other arithmetic: 237 us -> 3 us
  waiting for transfers between devices: 233 us -> 0.04 us
  matrix products: 167 us -> 21.7 us
  local copies, waits for them, and re-layouts: 140 us -> 22.9 us
    pallas_call x0 -> x11, Pallas kernels: none -> 312 us  [the longest x1 77.4 us: sum_col(): pl.pallas_call(functools.partial(sum_col_kernel, n_col), out_shape=jax.Sh...]
    another operation x39 -> x0, other arithmetic: 225 us -> none  [the longest x14 72.6 us: general_inverse(): lower = jnp.linalg.cholesky(matmul(square, square.T))]
    psum x5 -> x1, waiting for transfers between devices: 149 us -> 0.02 us  [on_device(): products = lax.psum(products, 'row')]
    dot_general x6 -> x1, matrix products: 109 us -> 5.11 us  [on_device(): jnp.dot(mine, mixed, precision=lax.Precision.HIGH, preferred_element_type...]
    unnamed x40 -> x27, local copies, waits for them, and re-layouts: 108 us -> 9.88 us
    reduce_scatter x1 -> x0, waiting for transfers between devices: 58.9 us -> none  [on_device(): lax.psum_scatter(jnp.concatenate([fast_matmul(amat, vectors_t.T), fast_ma...]
    dot_general x22 -> x7, matrix products: 42.6 us -> 16.6 us  [matmul(): jnp.dot(left, right, precision=lax.Precision.HIGHEST, preferred_element_t...]
    all_gather x1 -> x0, waiting for transfers between devices: 24.6 us -> none  [on_device(): gathered = lax.all_gather(scaled, 'col', axis=0, tiled=True)]
  transfers between devices with their start and end apart: 7 -> 1, of which waited for: 5 -> 0; matrix products, arithmetic and copies ran while one was open for 42% -> 2% of each run, Pallas kernels for 0% -> 38%
where the time goes in v1:
time: 375 us; the launch traced here: 374 us
  Pallas kernels  312 us (83%)
  local copies, waits for them, and re-layouts  22.9 us (6%)
  matrix products  21.7 us (6%)
  between operations  14.3 us (4%)
    pallas_call x1, Pallas kernels, sum_col(): pl.pallas_call(functools.partial(sum_col_kernel, n_col), out_shape=jax.Sh...  77.4 us
    pallas_call x1, Pallas kernels, broadcast_pair(): pl.pallas_call(functools.partial(broadcast_kernel, n_row, n_col, chunks),...  54.9 us
    pallas_call x2, Pallas kernels, update(): pl.pallas_call(functools.partial(update_kernel, rows_blk, per_row), grid=...  42.6 us
    pallas_call x1, Pallas kernels, share_grams(): pl.pallas_call(functools.partial(grams_kernel, n_row, n_col), out_shape=(...  33.6 us
    pallas_call x1, Pallas kernels, inverse_pair(): pl.pallas_call(functools.partial(inverse_kernel, 16), out_shape=jax.Shape...  23.8 us
    pallas_call x2, Pallas kernels, left_products(): pl.pallas_call(functools.partial(left_products_kernel, rows_blk, per_row)...  22.4 us
    pallas_call x1, Pallas kernels, right_products(): pl.pallas_call(functools.partial(right_products_kernel, rows_blk, per_row...  20.9 us
    pallas_call x1, Pallas kernels, sum_cross(): pl.pallas_call(functools.partial(cross_kernel, n_row, n_col), out_shape=j...  19 us
  transfers between devices with their start and end apart: 1, of which 0 were waited for; matrix products, arithmetic and copies ran while one was open for 2% of the time, Pallas kernels for 38%

profile of v1, /device:TPU:0, one launch (start us, length us, event | category | flops | bytes accessed | tf_op | source)
XLA Modules:
  0.0 373.9 jit_solution(8344985125671119673)
XLA Ops:
  7.2 0.0 all-reduce.5.cloned.1.call-start
  7.2 2.5 slice.36
  9.7 1.5 fusion.12.g2
  11.2 0.1 copy.25
  11.3 1.1 slice.37
  12.4 4.7 %slice.35 = f32[1,3072,1,256]{3,2,1,0:T(1,128)S(1)} slice(f32[1,3072,1,1536]{3,2,1,0:T(1,128)} %param.2), slice={[0:1], [0:3072], [0:1], [0:256]} | slice | bytes 6291456 | tf_op jit(solution)/shard_map/slice | solution.py:740
  17.1 5.4 %fusion.13.g1 = f32[256,256]{1,0:T(8,128)S(1)} fusion(f32[1,3072,1,256]{3,2,1,0:T(1,128)S(1)} %slice.35), kind=kOutput, calls=%fused_computation.32 | convolution fusion | flops 2415919104 | bytes 3407872 | tf_op jit(solution)/shard_map/dot_general | solution.py:18
  22.5 1.9 copy.24
  24.4 54.9 %broadcast_pair.1 = (f32[3072,256]{1,0:T(8,128)}, f32[256,1536]{1,0:T(8,128)S(1)}) custom-call(f32[3072,256]{1,0:T(8,128)} %bitcast.41, f32[256,1536]{1,0:T(8,128)S(1)} %bitcast.38), custom_call_target="tpu_custom_call" | custom-call | flops 10000000000 | bytes 10000000 | tf_op jit(solution)/shard_map/broadcast_pair/pallas_call | solution.py:420
  79.3 0.0 copy-start.3
  79.3 1.1 copy-done.3
  80.5 33.6 %share_grams.1 = (f32[2,256,256]{2,1,0:T(8,128)S(1)}, f32[2,256,256]{2,1,0:T(8,128)S(1)}) custom-call(f32[256,256]{1,0:T(8,128)S(1)} %fusion.13.g1, f32[256,256]{1,0:T(8,128)S(1)} %bitcast.39, f32[256,256]{1,0:T(8,128)S(1)} %fusion.12.g2, f32[256,256]{1,0:T(8,128)S(1)} %slice.46.ce), custom_call_target="tpu_custom_call" | custom-call | flops 5000000000 | bytes 1000000 | tf_op jit(solution)/shard_map/share_grams/pallas_call | solution.py:562
  114.0 0.0 copy-start
  114.1 0.8 copy-done
  114.8 0.0 copy-start.5
  114.8 0.8 copy-done.5
  115.6 0.0 copy-start.8
  115.6 17.3 %cholesky_pair.1.lower_ref = f32[2,256,256]{2,1,0:T(8,128)} custom-call(f32[2,256,256]{2,1,0:T(8,128)} %copy-done), custom_call_target="tpu_custom_call" | custom-call | flops 100000000 | bytes 1000000 | tf_op jit(solution)/shard_map/cholesky_pair/pallas_call | solution.py:238
  133.0 1.9 fusion.14
  134.8 1.1 copy.17
  135.9 0.0 copy-done.8
  135.9 1.9 pad_add_fusion.v_ref
  137.9 2.4 copy.10.pt_ref
  140.2 11.2 %left_products.3 = f32[256,1536]{1,0:T(8,128)S(1)} custom-call(f32[256,3072]{1,0:T(8,128)S(1)} %copy.10.pt_ref, f32[36864,128]{1,0:T(8,128)} %bitcast.45), custom_call_target="tpu_custom_call" | custom-call | flops 7247757312 | bytes 18874368 | tf_op jit(solution)/shard_map/left_products/pallas_call | solution.py:64
  151.5 0.0 copy-start.1
  151.5 1.2 copy-done.1
  152.6 11.2 %left_products.2 = f32[256,1536]{1,0:T(8,128)S(1)} custom-call(f32[256,3072]{1,0:T(8,128)S(1)} %copy.10.pt_ref, f32[36864,128]{1,0:T(8,128)} %bitcast.42), custom_call_target="tpu_custom_call" | custom-call | flops 7247757312 | bytes 18874368 | tf_op jit(solution)/shard_map/left_products/pallas_call | solution.py:64
  163.8 0.0 copy-start.2
  163.9 1.1 copy-done.2
  165.0 0.0 copy-start.10
  165.0 0.0 copy-start.4
  165.0 0.0 all-reduce.5.cloned.1.call-update
  165.0 0.9 copy-done.10
  165.9 0.8 copy.18
  166.8 0.0 copy-done.4
  166.8 0.5 copy.9
  167.3 0.2 fusion.2
  167.5 20.9 %right_products.1.part = f32[3072,512]{1,0:T(8,128)} custom-call(bf16[1536,256]{1,0:T(8,128)(2,1)S(1)} %get-tuple-element.19.whi_ref, bf16[1536,256]{1,0:T(8,128)(2,1)S(1)} %get-tuple-element.18.wlo_ref, f32[36864,128]{1,0:T(8,128)} %bitcast.43, f32[36864,128]{1,0:T(8,128)} %bitcast.46), custom_call_target="tpu_custom_call" | custom-call | flops 14495514624 | bytes 37748736 | tf_op jit(solution)/shard_map/right_products/pallas_call | solution.py:100
  188.5 23.8 %inverse_pair.1 = f32[2,256,256]{2,1,0:T(8,128)} custom-call(f32[2,256,256]{2,1,0:T(8,128)} %copy-done, f32[2,256,256]{2,1,0:T(8,128)} %cholesky_pair.1.lower_ref, f32[2,256,256]{2,1,0:T(8,128)} %copy-done.5), custom_call_target="tpu_custom_call" | custom-call | flops 100000000 | bytes 1000000 | tf_op jit(solution)/shard_map/inverse_pair/pallas_call | solution.py:280
  212.3 2.4 fusion.5
  214.7 0.0 copy-start.6
  214.7 77.4 %sum_col.1.s_ref = f32[3072,512]{1,0:T(8,128)} custom-call(f32[3072,512]{1,0:T(8,128)} %right_products.1.part), custom_call_target="tpu_custom_call" | custom-call | flops 20000000000 | bytes 10000000 | tf_op jit(solution)/shard_map/sum_col/pallas_call | solution.py:714
  292.1 0.0 copy-done.6
  292.1 5.1 %fusion.3.mine = f32[32,512]{1,0:T(8,128)S(1)} fusion(f32[3072,512]{1,0:T(8,128)} %sum_col.1.s_ref, f32[3072,256]{1,0:T(8,128)S(1)} %copy-done.6, s32[]{:T(128)S(6)} %select_n.33), kind=kOutput, calls=%fused_computation.16 | convolution fusion | flops 301989888 | bytes 7929860 | tf_op jit(solution)/shard_map/dot_general | solution.py:764
  297.2 19.0 %sum_cross.1 = f32[256,512]{1,0:T(8,128)S(1)} custom-call(f32[32,512]{1,0:T(8,128)S(1)} %fusion.3.mine), custom_call_target="tpu_custom_call" | custom-call | flops 5000000000 | bytes 1000000 | tf_op jit(solution)/shard_map/sum_cross/pallas_call | solution.py:621
  316.2 0.0 all-reduce.5.cloned.1.call-done
  316.2 0.0 copy-start.9
  316.2 3.0 convolution_subtract_fusion
  319.3 0.0 copy-done.9
  319.3 0.0 copy-start.7
  319.3 1.4 convolution_subtract_fusion.1
  320.7 0.0 copy-done.7
  320.7 1.4 fusion.9
  322.2 1.4 fusion.8
  323.6 0.8 fusion.1
  324.5 21.5 %update.3 = f32[36864,128]{1,0:T(8,128)} custom-call(f32[3072,256]{1,0:T(8,128)} %pad_add_fusion.v_ref, f32[3072,512]{1,0:T(8,128)} %sum_col.1.s_ref, bf16[512,1536]{1,0:T(8,128)(2,1)S(1)} %get-tuple-element.15.dhi_ref, bf16[512,1536]{1,0:T(8,128)(2,1)S(1)} %get-tuple-element.14.dlo_ref, f32[36864,128]{1,0:T(8,128)} %bitcast.47), custom_call_target="tpu_custom_call" | custom-call | flops 14495514624 | bytes 37748736 | tf_op jit(solution)/shard_map/update/pallas_call | solution.py:136
  345.9 21.2 %update.2 = f32[36864,128]{1,0:T(8,128)} custom-call(f32[3072,256]{1,0:T(8,128)} %pad_add_fusion.v_ref, f32[3072,512]{1,0:T(8,128)} %sum_col.1.s_ref, bf16[512,1536]{1,0:T(8,128)(2,1)S(1)} %get-tuple-element.20.dhi_ref, bf16[512,1536]{1,0:T(8,128)(2,1)S(1)} %get-tuple-element.21.dlo_ref, f32[36864,128]{1,0:T(8,128)} %bitcast.44), custom_call_target="tpu_custom_call" | custom-call | flops 14495514624 | bytes 37748736 | tf_op jit(solution)/shard_map/update/pallas_call | solution.py:136
  (4 shorter events, 0.1 us)
Async XLA Ops:
  7.2 309.1 %all-reduce.5.cloned.1.call-start = ((), (), s32[]{:S(2)}) async-start(), calls=%async_computation | async-start | bytes 6291456 | tf_op jit(solution)/shard_map/psum | solution.py:759
  79.3 1.1 copy-start.3
  114.0 0.8 copy-start
  114.8 0.8 copy-start.5
  115.6 20.3 %copy-start.8 = (f32[3072,256]{1,0:T(8,128)S(1)}, f32[3072,256]{1,0:T(8,128)}, u32[]{:S(2)}) copy-start(f32[3072,256]{1,0:T(8,128)} %get-tuple-element.6) | copy-start | bytes 9437188
  151.5 1.2 copy-start.1
  163.8 1.1 copy-start.2
  165.0 0.9 copy-start.10
  165.0 1.8 copy-start.4
  214.7 77.4 %copy-start.6 = (f32[3072,256]{1,0:T(8,128)S(1)}, f32[3072,256]{1,0:T(8,128)}, u32[]{:S(2)}) copy-start(f32[3072,256]{1,0:T(8,128)} %pad_add_fusion.v_ref) | copy-start | bytes 9437188
  316.2 3.0 copy-start.9
  319.3 1.5 copy-start.7
Sparse Core Ops, SparseCore 0:
  165.1 130.2 all-reduce.4
